TPU v7x, 32 devices: a whole 2x2x4 slice. The times are simulated.
32 devices in a mesh: row: 8 (over z, x), col: 4 (over y, core).
Axes of the slice: x: 2, y: 2, z: 4, core: 2. Of those that a mesh axis runs over, the one named last changes fastest.
Arguments:
- matrix: float32 [5, 8, 10, 4, 128, 128], P(None, 'row', None, 'col'), may hold values from 0 to 2.5, as said below
- flags: int32 [5, 8, 10, 4], P(None, 'row', None, 'col'), may hold values from 0 to 1, as said below
Outputs:
- factor: float32 [5, 8, 10, 4, 128, 128], P(None, 'row', None, 'col')
Inputs may be any that keep to these rules, and one draw needn't show every extreme that they name: `matrix`: symmetric positive definite, of order 40*128, diagonal at least 1.5. `flags`: 0 marks a float32 tile, 1 a bfloat16 tile; every diagonal tile is 0.
All inputs are finite; a program needn't handle non-finite values.
Results may differ from a plain program's by a relative error of at most 0.0005.
The roundings to bfloat16 on the way count: a program that leaves them out, or rounds other values in their place, can miss the bound.
Values sent between devices are 32-bit elements; how exact they have to be, the bound alone decides.
No kernel may reach another device: no remote copies, remote signals or barrier semaphores. Data moves between devices by JAX's collectives and lax.ppermute only.
A program may use at most 128 MiB of HBM per device.

v0:
```python
import jax
import jax.numpy as jnp
from jax import lax
from jax.sharding import PartitionSpec as P

PT = 4


def spread(value, axis, source):
    kept = jnp.where(lax.axis_index(axis) == source, value, 0).astype(value.dtype)
    return lax.psum(kept, axis)


def storage_round(values):
    narrow = lax.optimization_barrier(values.astype(jnp.bfloat16))
    return narrow.astype(jnp.float32)


def solve_rows(lower_block, rows):
    width = rows.shape[2]
    flat = rows.reshape(-1, width)
    solved = jax.scipy.linalg.solve_triangular(lower_block, flat.T, lower=True).T
    return solved.reshape(rows.shape)


def with_block(solved, lower_block, global_ids, start):
    offset = jnp.clip(global_ids - start, 0, PT - 1)
    block_rows = lower_block.reshape(PT, solved.shape[1], solved.shape[2])[offset]
    inside = (global_ids >= start) & (global_ids < start + PT)
    return jnp.where(inside[:, None, None], block_rows, solved)


def factor_panel(work, start, row_ids, row_count, col_count):
    pieces = []
    for column in range(start, start + PT):
        pieces.append(spread(work[:, column // col_count], "col", column % col_count))
    panel_rows = jnp.concatenate(pieces, axis=2)
    blocks = []
    for tile_row in range(start, start + PT):
        blocks.append(spread(panel_rows[tile_row // row_count], "row", tile_row % row_count))
    dense = jnp.concatenate(blocks, axis=0)
    sym = jnp.tril(dense) + jnp.tril(dense, -1).T
    lower_block = jnp.linalg.cholesky(sym)
    solved = with_block(solve_rows(lower_block, panel_rows), lower_block, row_ids, start)
    return (panel_rows, lower_block, solved)


def apply_update(work, marks, left, right, row_ids, col_ids, low, high):
    exact = jnp.einsum("aik,cjk->acij", left, right, precision=lax.Precision.HIGHEST)
    coarse = jnp.einsum(
        "aik,cjk->acij",
        left.astype(jnp.bfloat16),
        right.astype(jnp.bfloat16),
        preferred_element_type=jnp.float32,
    )
    live = (
        (row_ids[:, None] >= col_ids[None, :])
        & (col_ids >= low)[None, :]
        & (col_ids < high)[None, :]
    )
    updated = jnp.where((marks == 1)[:, :, None, None], work - coarse, work - exact)
    return jnp.where(live[:, :, None, None], updated, work)


def store_panel(work, solved, start, row_ids, col_index, col_count):
    tile = work.shape[2]
    for column in range(start, start + PT):
        slot = column // col_count
        offset = column - start
        piece = solved[:, :, offset * tile : (offset + 1) * tile]
        keep = (row_ids >= start)[:, None, None] & (col_index == column % col_count)
        work = work.at[:, slot].set(jnp.where(keep, piece, work[:, slot]))
    return work


def on_device(matrix, flags):
    row_count = lax.axis_size("row")
    col_count = lax.axis_size("col")
    row_index = lax.axis_index("row")
    col_index = lax.axis_index("col")
    tile_rows = matrix.shape[0]
    tile_cols = matrix.shape[2]
    tile = matrix.shape[4]
    tiles = matrix.reshape(tile_rows, tile_cols, tile, tile)
    marks = flags.reshape(tile_rows, tile_cols)
    row_ids = jnp.arange(tile_rows, dtype=jnp.int32) * row_count + row_index
    col_ids = jnp.arange(tile_cols, dtype=jnp.int32) * col_count + col_index
    work = jnp.where((marks == 1)[:, :, None, None], storage_round(tiles), tiles)
    beyond = 1 << 30
    lefts = []
    rights = []
    for step in range(2):
        start = step * PT
        panel_rows, lower_block, solved = factor_panel(work, start, row_ids, row_count, col_count)
        received = []
        for slot in range(tile_cols):
            column = col_ids[slot]
            piece = lax.dynamic_index_in_dim(solved, column // row_count, 0, keepdims=False)
            received.append(spread(piece, "row", column % row_count))
        right = jnp.stack(received, axis=0)
        lefts.append(solved)
        rights.append(right)
        work = apply_update(work, marks, solved, right, row_ids, col_ids, start + PT, beyond)
        work = store_panel(work, solved, start, row_ids, col_index, col_count)
    final = jnp.where((marks == 1)[:, :, None, None], storage_round(work), work)
    upper = row_ids[:, None] < col_ids[None, :]
    final = jnp.where(upper[:, :, None, None], jnp.float32(0.0), final)
    return final.reshape(matrix.shape)


def solution(mesh):
    return jax.shard_map(
        on_device,
        mesh=mesh,
        in_specs=(P(None, "row", None, "col", None, None), P(None, "row", None, "col")),
        out_specs=P(None, "row", None, "col", None, None),
        check_vma=False,
    )
```

profile of v0, /device:TPU:0, one launch (start us, length us, event | category | flops | bytes accessed | tf_op | source)
XLA Modules:
  0.0 841.9 jit_solution(16314671458284499943)
XLA Ops:
  7.5 2.2 copy.42
  10.1 1.7 copy-done.2
  11.8 1.1 select_bitcast_fusion.5
  13.0 42.1 %all-reduce.24.cloned.1.call-done = (f32[5,128,128]{2,1,0:T(8,128)}, f32[5,128,128]{2,1,0:T(8,128)}, f32[5,128,128]{2,1,0:T(8,128)}, f32[5,128,128]{2,1,0:T(8,128)}) async-done(((f32[5,128,128]{2,1,0:T(8,128)}, f32[5,128,128]{2,1,0:T(8,128)}, f32[5,128,128]{2,1,0:T(8,128)}, f32[5,128,128]{2,1,0:T(8,128)}), (f32[5,128,128]{2,1,0:T(8,128)}, f32[5,128,128]{2,1,0:T(8,128)}, f32[5,128,128]{2,1,0:T(8,128)}, ...) | async-done | bytes 1310736 | tf_op jit(solution)/shard_map/psum | solution.py:11
  59.1 1.1 copy-done.5
  87.3 52.5 %all-reduce.20.cloned.1.call-done = (f32[128,512]{1,0:T(8,128)}, f32[128,512]{1,0:T(8,128)}, f32[128,512]{1,0:T(8,128)}, f32[128,512]{1,0:T(8,128)}) async-done(((f32[128,512]{1,0:T(8,128)}, f32[128,512]{1,0:T(8,128)}, f32[128,512]{1,0:T(8,128)}, f32[128,512]{1,0:T(8,128)}), (f32[128,512]{1,0:T(8,128)}, f32[128,512]{1,0:T(8,128)}, f32[128,512]{1,0:T(8,128)}, ...) | async-done | bytes 1048592 | tf_op jit(solution)/shard_map/psum | solution.py:11
  144.8 11.7 %cholesky.286 = f32[128,128]{1,0:T(8,128)S(1)} custom-call(f32[128,128]{1,0:T(8,128)S(1)} %cholesky.426), custom_call_target="Cholesky" | custom-call | tf_op jit(solution)/shard_map/jit(cholesky)/cholesky | solution.py:43
  156.7 9.8 %custom-call.27 = f32[1,128,128]{1,2,0:T(8,128)S(1)} custom-call(f32[1,128,128]{2,1,0:T(8,128)S(1)} %get-tuple-element.236), custom_call_target="InvertDiagBlocksLowerTriangular" | custom-call | tf_op jit(solution)/shard_map/jit(cholesky)/cholesky | solution.py:43
  167.2 11.7 %cholesky.305 = f32[128,128]{1,0:T(8,128)S(1)} custom-call(f32[128,128]{1,0:T(8,128)S(1)} %cholesky.430), custom_call_target="Cholesky" | custom-call | tf_op jit(solution)/shard_map/jit(cholesky)/cholesky | solution.py:43
  179.0 9.9 %custom-call.28 = f32[1,128,128]{1,2,0:T(8,128)S(1)} custom-call(f32[1,128,128]{2,1,0:T(8,128)S(1)} %get-tuple-element.233), custom_call_target="InvertDiagBlocksLowerTriangular" | custom-call | tf_op jit(solution)/shard_map/jit(cholesky)/cholesky | solution.py:43
  189.5 11.7 %cholesky.326 = f32[128,128]{1,0:T(8,128)S(1)} custom-call(f32[128,128]{1,0:T(8,128)S(1)} %cholesky.435), custom_call_target="Cholesky" | custom-call | tf_op jit(solution)/shard_map/jit(cholesky)/cholesky | solution.py:43
  202.0 9.8 %custom-call.29 = f32[1,128,128]{1,2,0:T(8,128)S(1)} custom-call(f32[1,128,128]{2,1,0:T(8,128)S(1)} %get-tuple-element.230), custom_call_target="InvertDiagBlocksLowerTriangular" | custom-call | tf_op jit(solution)/shard_map/jit(cholesky)/cholesky | solution.py:43
  212.4 11.9 %cholesky.343 = f32[128,128]{1,0:T(8,128)S(1)} custom-call(f32[128,128]{1,0:T(8,128)S(1)} %convolution_subtract_fusion.11), custom_call_target="Cholesky" | custom-call | tf_op jit(solution)/shard_map/jit(cholesky)/cholesky | solution.py:43
  228.6 8.1 while.12
  229.3 1.3 bitcast_dynamic-update-slice_fusion.10
  231.3 1.3 bitcast_dynamic-update-slice_fusion.10
  233.3 1.3 bitcast_dynamic-update-slice_fusion.10
  235.4 1.3 bitcast_dynamic-update-slice_fusion.10
  236.7 39.3 %custom-call.30 = f32[4,128,128]{1,2,0:T(8,128)S(1)} custom-call(f32[4,128,128]{2,1,0:T(8,128)S(1)} %get-tuple-element.117), custom_call_target="InvertDiagBlocksLowerTriangular" | custom-call | tf_op jit(solution)/shard_map/jit(_solve_triangular)/triangular_solve | solution.py:22
  276.0 1.5 fusion.46
  277.5 1.7 convolution_subtract_fusion.3
  279.7 2.2 convolution_subtract_fusion.2
  282.4 2.7 convolution_subtract_fusion.5
  285.6 1.2 maximum_bitcast_fusion
  286.8 1.7 copy.9
  288.5 1.7 gather_fusion
  290.3 1.6 broadcast_select_fusion.1
  292.6 1.5 dynamic-slice_select_fusion.10
  294.8 115.8 %all-reduce.18.cloned.1.call-done = (f32[1,128,512]{2,1,0:T(8,128)}, f32[1,128,512]{2,1,0:T(8,128)}, f32[1,128,512]{2,1,0:T(8,128)}, f32[1,128,512]{2,1,0:T(8,12...) async-done(((f32[1,128,512]{2,1,0:T(8,128)}, ...) | async-done | bytes 2621456 | tf_op jit(solution)/shard_map/psum | solution.py:11
  410.6 1.1 constant_dynamic-update-slice_fusion.17
  415.8 5.4 fusion.6
  421.2 1.3 fusion.3
  423.0 1.7 copy-done
  424.7 1.1 select_bitcast_fusion.1
  425.9 38.2 %all-reduce.22.cloned.1.call-done = (f32[5,128,128]{2,1,0:T(8,128)}, f32[5,128,128]{2,1,0:T(8,128)}, f32[5,128,128]{2,1,0:T(8,128)}, f32[5,128,128]{2,1,0:T(8,128)}) async-done(((f32[5,128,128]{2,1,0:T(8,128)}, f32[5,128,128]{2,1,0:T(8,128)}, f32[5,128,128]{2,1,0:T(8,128)}, f32[5,128,128]{2,1,0:T(8,128)}), (f32[5,128,128]{2,1,0:T(8,128)}, f32[5,128,128]{2,1,0:T(8,128)}, f32[5,128,128]{2,1,0:T(8,128)}, ...) | async-done | bytes 1310736 | tf_op jit(solution)/shard_map/psum | solution.py:11
  468.1 1.1 copy-done.6
  471.0 77.9 %all-reduce.16.cloned.1.call-done = (f32[128,512]{1,0:T(8,128)}, f32[128,512]{1,0:T(8,128)}, f32[128,512]{1,0:T(8,128)}, f32[128,512]{1,0:T(8,128)}) async-done(((f32[128,512]{1,0:T(8,128)}, f32[128,512]{1,0:T(8,128)}, f32[128,512]{1,0:T(8,128)}, f32[128,512]{1,0:T(8,128)}), (f32[128,512]{1,0:T(8,128)}, f32[128,512]{1,0:T(8,128)}, f32[128,512]{1,0:T(8,128)}, ...) | async-done | bytes 1048592 | tf_op jit(solution)/shard_map/psum | solution.py:11
  554.0 11.7 %cholesky.358 = f32[128,128]{1,0:T(8,128)S(1)} custom-call(f32[128,128]{1,0:T(8,128)S(1)} %cholesky.439), custom_call_target="Cholesky" | custom-call | tf_op jit(solution)/shard_map/jit(cholesky)/cholesky | solution.py:43
  565.9 9.8 %custom-call.31 = f32[1,128,128]{1,2,0:T(8,128)S(1)} custom-call(f32[1,128,128]{2,1,0:T(8,128)S(1)} %get-tuple-element.226), custom_call_target="InvertDiagBlocksLowerTriangular" | custom-call | tf_op jit(solution)/shard_map/jit(cholesky)/cholesky | solution.py:43
  576.4 11.7 %cholesky.377 = f32[128,128]{1,0:T(8,128)S(1)} custom-call(f32[128,128]{1,0:T(8,128)S(1)} %cholesky.443), custom_call_target="Cholesky" | custom-call | tf_op jit(solution)/shard_map/jit(cholesky)/cholesky | solution.py:43
  589.8 9.8 %custom-call.32 = f32[1,128,128]{1,2,0:T(8,128)S(1)} custom-call(f32[1,128,128]{2,1,0:T(8,128)S(1)} %get-tuple-element.223), custom_call_target="InvertDiagBlocksLowerTriangular" | custom-call | tf_op jit(solution)/shard_map/jit(cholesky)/cholesky | solution.py:43
  600.3 11.7 %cholesky.398 = f32[128,128]{1,0:T(8,128)S(1)} custom-call(f32[128,128]{1,0:T(8,128)S(1)} %cholesky.448), custom_call_target="Cholesky" | custom-call | tf_op jit(solution)/shard_map/jit(cholesky)/cholesky | solution.py:43
  612.7 9.8 %custom-call.33 = f32[1,128,128]{1,2,0:T(8,128)S(1)} custom-call(f32[1,128,128]{2,1,0:T(8,128)S(1)} %get-tuple-element.220), custom_call_target="InvertDiagBlocksLowerTriangular" | custom-call | tf_op jit(solution)/shard_map/jit(cholesky)/cholesky | solution.py:43
  623.1 11.9 %cholesky.415 = f32[128,128]{1,0:T(8,128)S(1)} custom-call(f32[128,128]{1,0:T(8,128)S(1)} %convolution_subtract_fusion.10), custom_call_target="Cholesky" | custom-call | tf_op jit(solution)/shard_map/jit(cholesky)/cholesky | solution.py:43
  638.4 7.3 while.13
  639.0 1.2 bitcast_dynamic-update-slice_fusion.11
  640.8 1.2 bitcast_dynamic-update-slice_fusion.11
  642.6 1.2 bitcast_dynamic-update-slice_fusion.11
  644.5 1.2 bitcast_dynamic-update-slice_fusion.11
  645.7 39.3 %custom-call.34 = f32[4,128,128]{1,2,0:T(8,128)S(1)} custom-call(f32[4,128,128]{2,1,0:T(8,128)S(1)} %get-tuple-element.118), custom_call_target="InvertDiagBlocksLowerTriangular" | custom-call | tf_op jit(solution)/shard_map/jit(_solve_triangular)/triangular_solve | solution.py:22
  685.0 1.5 fusion.41
  686.5 1.7 convolution_subtract_fusion.1
  688.7 2.2 convolution_subtract_fusion
  691.4 2.7 convolution_subtract_fusion.4
  694.6 1.2 maximum_bitcast_fusion.1
  695.8 1.7 copy.15
  697.5 1.7 gather_fusion.1
  699.2 1.6 broadcast_select_fusion
  700.9 1.5 dynamic-slice_select_fusion
  703.2 116.4 %all-reduce.14.cloned.1.call-done = (f32[1,128,512]{2,1,0:T(8,128)}, f32[1,128,512]{2,1,0:T(8,128)}, f32[1,128,512]{2,1,0:T(8,128)}, f32[1,128,512]{2,1,0:T(8,12...) async-done(((f32[1,128,512]{2,1,0:T(8,128)}, ...) | async-done | bytes 2621456 | tf_op jit(solution)/shard_map/psum | solution.py:11
  819.6 1.1 constant_dynamic-update-slice_fusion.35
  824.8 5.6 fusion.4
  830.4 1.3 fusion.1
  832.9 1.9 copy.18
  (186 shorter events, 52.9 us)
Async XLA Ops:
  6.5 3.2 copy-start.4
  6.5 48.5 %all-reduce.24.cloned.1.call-start = ((), (), s32[]{:S(2)}) async-start(), calls=%async_computation.5 | async-start | bytes 2621440 | tf_op jit(solution)/shard_map/psum | solution.py:11
  10.1 1.7 copy-start.2
  12.9 126.9 %all-reduce.20.cloned.1.call-start = ((), (), s32[]{:S(2)}) async-start(), calls=%async_computation.3 | async-start | bytes 2097152 | tf_op jit(solution)/shard_map/psum | solution.py:11
  59.1 1.1 copy-start.5
  61.3 349.3 %all-reduce.18.cloned.1.call-start = ((), (), s32[]{:S(2)}) async-start(), calls=%async_computation.2 | async-start | bytes 5242880 | tf_op jit(solution)/shard_map/psum | solution.py:11
  294.1 169.9 %all-reduce.22.cloned.1.call-start = ((), (), s32[]{:S(2)}) async-start(), calls=%async_computation.4 | async-start | bytes 2621440 | tf_op jit(solution)/shard_map/psum | solution.py:11
  410.6 5.0 copy-start.11
  410.6 5.0 copy-start.10
  410.6 5.1 copy-start.9
  410.6 5.1 copy-start.8
  410.6 5.1 copy-start.7
  415.8 5.4 copy-start.3
  423.0 1.7 copy-start
  425.8 123.0 %all-reduce.16.cloned.1.call-start = ((), (), s32[]{:S(2)}) async-start(), calls=%async_computation.1 | async-start | bytes 2097152 | tf_op jit(solution)/shard_map/psum | solution.py:11
  468.1 1.1 copy-start.6
  470.2 349.3 %all-reduce.14.cloned.1.call-start = ((), (), s32[]{:S(2)}) async-start(), calls=%async_computation | async-start | bytes 5242880 | tf_op jit(solution)/shard_map/psum | solution.py:11
  819.6 5.0 copy-start.16
  819.6 5.0 copy-start.15
  819.6 5.1 copy-start.14
  819.6 5.1 copy-start.13
  819.6 5.1 copy-start.12
  824.7 5.6 copy-start.1
Sparse Core Ops, SparseCore 0:
  13.0 41.9 all-reduce.23
  61.4 78.4 all-reduce.19
  294.3 116.2 all-reduce.17
  425.9 38.0 all-reduce.21
  470.4 78.4 all-reduce.15
  703.2 116.2 all-reduce.13
where the time goes:
time: 853 us; the launch traced here: 842 us
  waiting for transfers between devices  443 us (52%)
  other arithmetic  256 us (30%)
  local copies, waits for them, and re-layouts  60.7 us (7%)
  between operations  45 us (5%)
  matrix products  36.4 us (4%)
    psum x6, waiting for transfers between devices, spread(): return lax.psum(kept, axis)  443 us
    another operation x29, other arithmetic, factor_panel(): lower_block = jnp.linalg.cholesky(sym)  158 us
    another operation x5, other arithmetic, solve_rows(): jax.scipy.linalg.solve_triangular(lower_block, flat.T, lower=True)  79.2 us
    unnamed x65, local copies, waits for them, and re-layouts  29.8 us
    another operation x14, matrix products, solve_rows(): jax.scipy.linalg.solve_triangular(lower_block, flat.T, lower=True)  19.1 us
  transfers between devices with their start and end apart: 6, of which 6 were waited for; matrix products, arithmetic and copies ran while one was open for 0% of the time, Pallas kernels for 0%

commit v1 on v0

--- a/solution.py
+++ b/solution.py
@@ -8,7 +8,7 @@
 
 def spread(value, axis, source):
     kept = jnp.where(lax.axis_index(axis) == source, value, 0).astype(value.dtype)
-    return lax.psum(kept, axis)
+    return jnp.sum(lax.all_gather(kept, axis), axis=0)
 
 
 def storage_round(values):

time: 853 us -> 1940 us (2.27)
  waiting for transfers between devices: 443 us -> 1410 us
  other arithmetic: 256 us -> 316 us
  local copies, waits for them, and re-layouts: 60.7 us -> 111 us
    all_gather x0 -> x36, waiting for transfers between devices: none -> 1410 us  [spread(): return jnp.sum(lax.all_gather(kept, axis), axis=0)]
    psum x6 -> x0, waiting for transfers between devices: 443 us -> none  [spread(): return lax.psum(kept, axis)]
    reduce_sum x0 -> x36, other arithmetic: none -> 63.7 us  [spread(): return jnp.sum(lax.all_gather(kept, axis), axis=0)]
    select_n x0 -> x36, local copies, waits for them, and re-layouts: none -> 32.8 us  [spread(): jnp.where(lax.axis_index(axis) == source, value, 0).astype(value.dtype)]
  transfers between devices with their start and end apart: 6 -> 36, of which waited for: 6 -> 36; matrix products, arithmetic and copies ran while one was open for 0% -> 5% of each run, Pallas kernels for 0% -> 0%
where the time goes in v1:
time: 1940 us; the launch traced here: 1930 us
  waiting for transfers between devices  1410 us (73%)
  other arithmetic  316 us (16%)
  local copies, waits for them, and re-layouts  111 us (6%)
  matrix products  46.7 us (2%)
  between operations  45.7 us (2%)
    all_gather x36, waiting for transfers between devices, spread(): return jnp.sum(lax.all_gather(kept, axis), axis=0)  1410 us
    another operation x29, other arithmetic, factor_panel(): lower_block = jnp.linalg.cholesky(sym)  158 us
    another operation x5, other arithmetic, solve_rows(): jax.scipy.linalg.solve_triangular(lower_block, flat.T, lower=True)  81.1 us
    reduce_sum x36, other arithmetic, spread(): return jnp.sum(lax.all_gather(kept, axis), axis=0)  63.7 us
  transfers between devices with their start and end apart: 36, of which 36 were waited for; matrix products, arithmetic and copies ran while one was open for 5% of the time, Pallas kernels for 0%

profile of v1, /device:TPU:0, one launch (start us, length us, event | category | flops | bytes accessed | tf_op | source)
XLA Modules:
  0.0 1932.0 jit_solution(10071410157549695500)
XLA Ops:
  7.3 3.5 copy.171
  17.2 18.1 all-gather.101.cloned.1.call-done
  36.9 18.2 all-gather.103.cloned.1.call-done
  56.7 18.2 all-gather.105.cloned.1.call-done
  76.4 18.0 all-gather.107.cloned.1.call-done
  127.3 19.1 all-gather.45.cloned.1.call-done
  148.4 47.7 %all-gather.47.cloned.1.call-done = f32[8,128,512]{2,1,0:T(8,128)} async-done(((f32[1,128,512]{2,1,0:T(8,128)}), f32[8,128,512]{2,1,0:T(8,128)}) %all-gather.47.cloned.1.call-update) | async-done | bytes 2097168 | tf_op jit(solution)/shard_map/all_gather | solution.py:11
  198.0 47.8 %all-gather.49.cloned.1.call-done = f32[8,128,512]{2,1,0:T(8,128)} async-done(((f32[1,128,512]{2,1,0:T(8,128)}), f32[8,128,512]{2,1,0:T(8,128)}) %all-gather.49.cloned.1.call-update) | async-done | bytes 2097168 | tf_op jit(solution)/shard_map/all_gather | solution.py:11
  247.8 47.8 %all-gather.51.cloned.1.call-done = f32[8,128,512]{2,1,0:T(8,128)} async-done(((f32[1,128,512]{2,1,0:T(8,128)}), f32[8,128,512]{2,1,0:T(8,128)}) %all-gather.51.cloned.1.call-update) | async-done | bytes 2097168 | tf_op jit(solution)/shard_map/all_gather | solution.py:11
  301.7 11.7 cholesky.286
  313.6 9.8 custom-call.27
  326.3 11.9 cholesky.305
  338.2 9.8 custom-call.28
  349.8 11.7 cholesky.326
  362.2 9.8 custom-call.29
  373.7 12.1 cholesky.343
  391.0 11.7 while.12
  402.7 39.3 %custom-call.30 = f32[4,128,128]{1,2,0:T(8,128)S(1)} custom-call(f32[4,128,128]{2,1,0:T(8,128)S(1)} %get-tuple-element.117), custom_call_target="InvertDiagBlocksLowerTriangular" | custom-call | tf_op jit(solution)/shard_map/jit(_solve_triangular)/triangular_solve | solution.py:22
  453.4 2.8 copy.201
  471.7 35.6 %all-gather.55.cloned.1.call-done = f32[8,128,512]{2,1,0:T(8,128)} async-done(((f32[1,128,512]{2,1,0:T(8,128)}), f32[8,128,512]{2,1,0:T(8,128)}) %all-gather.55.cloned.1.call-update) | async-done | bytes 2097168 | tf_op jit(solution)/shard_map/all_gather | solution.py:11
  509.1 47.8 %all-gather.53.cloned.1.call-done = f32[8,128,512]{2,1,0:T(8,128)} async-done(((f32[1,128,512]{2,1,0:T(8,128)}), f32[8,128,512]{2,1,0:T(8,128)}) %all-gather.53.cloned.1.call-update) | async-done | bytes 2097168 | tf_op jit(solution)/shard_map/all_gather | solution.py:11
  558.7 48.0 %all-gather.57.cloned.1.call-done = f32[8,128,512]{2,1,0:T(8,128)} async-done(((f32[1,128,512]{2,1,0:T(8,128)}), f32[8,128,512]{2,1,0:T(8,128)}) %all-gather.57.cloned.1.call-update) | async-done | bytes 2097168 | tf_op jit(solution)/shard_map/all_gather | solution.py:11
  608.5 47.8 %all-gather.59.cloned.1.call-done = f32[8,128,512]{2,1,0:T(8,128)} async-done(((f32[1,128,512]{2,1,0:T(8,128)}), f32[8,128,512]{2,1,0:T(8,128)}) %all-gather.59.cloned.1.call-update) | async-done | bytes 2097168 | tf_op jit(solution)/shard_map/all_gather | solution.py:11
  658.1 48.0 %all-gather.61.cloned.1.call-done = f32[8,128,512]{2,1,0:T(8,128)} async-done(((f32[1,128,512]{2,1,0:T(8,128)}), f32[8,128,512]{2,1,0:T(8,128)}) %all-gather.61.cloned.1.call-update) | async-done | bytes 2097168 | tf_op jit(solution)/shard_map/all_gather | solution.py:11
  707.9 47.8 %all-gather.63.cloned.1.call-done = f32[8,128,512]{2,1,0:T(8,128)} async-done(((f32[1,128,512]{2,1,0:T(8,128)}), f32[8,128,512]{2,1,0:T(8,128)}) %all-gather.63.cloned.1.call-update) | async-done | bytes 2097168 | tf_op jit(solution)/shard_map/all_gather | solution.py:11
  757.5 47.8 %all-gather.65.cloned.1.call-done = f32[8,128,512]{2,1,0:T(8,128)} async-done(((f32[1,128,512]{2,1,0:T(8,128)}), f32[8,128,512]{2,1,0:T(8,128)}) %all-gather.65.cloned.1.call-update) | async-done | bytes 2097168 | tf_op jit(solution)/shard_map/all_gather | solution.py:11
  807.2 47.8 %all-gather.67.cloned.1.call-done = f32[8,128,512]{2,1,0:T(8,128)} async-done(((f32[1,128,512]{2,1,0:T(8,128)}), f32[8,128,512]{2,1,0:T(8,128)}) %all-gather.67.cloned.1.call-update) | async-done | bytes 2097168 | tf_op jit(solution)/shard_map/all_gather | solution.py:11
  856.8 47.8 %all-gather.69.cloned.1.call-done = f32[8,128,512]{2,1,0:T(8,128)} async-done(((f32[1,128,512]{2,1,0:T(8,128)}), f32[8,128,512]{2,1,0:T(8,128)}) %all-gather.69.cloned.1.call-update) | async-done | bytes 2097168 | tf_op jit(solution)/shard_map/all_gather | solution.py:11
  904.6 2.5 reduce_sum.340
  913.6 40.6 %all-gather.71.cloned.1.call-done = f32[8,128,512]{2,1,0:T(8,128)} async-done(((f32[1,128,512]{2,1,0:T(8,128)}), f32[8,128,512]{2,1,0:T(8,128)}) %all-gather.71.cloned.1.call-update) | async-done | bytes 2097168 | tf_op jit(solution)/shard_map/all_gather | solution.py:11
  956.8 8.3 fusion.6
  965.1 2.9 fusion.3
  974.3 13.9 all-gather.109.cloned.1.call-done
  989.8 18.0 all-gather.111.cloned.1.call-done
  1009.4 18.2 all-gather.113.cloned.1.call-done
  1029.2 18.2 all-gather.115.cloned.1.call-done
  1057.7 41.5 %all-gather.73.cloned.1.call-done = f32[8,128,512]{2,1,0:T(8,128)} async-done(((f32[1,128,512]{2,1,0:T(8,128)}), f32[8,128,512]{2,1,0:T(8,128)}) %all-gather.73.cloned.1.call-update) | async-done | bytes 2097168 | tf_op jit(solution)/shard_map/all_gather | solution.py:11
  1101.0 47.8 %all-gather.75.cloned.1.call-done = f32[8,128,512]{2,1,0:T(8,128)} async-done(((f32[1,128,512]{2,1,0:T(8,128)}), f32[8,128,512]{2,1,0:T(8,128)}) %all-gather.75.cloned.1.call-update) | async-done | bytes 2097168 | tf_op jit(solution)/shard_map/all_gather | solution.py:11
  1150.7 47.9 %all-gather.77.cloned.1.call-done = f32[8,128,512]{2,1,0:T(8,128)} async-done(((f32[1,128,512]{2,1,0:T(8,128)}), f32[8,128,512]{2,1,0:T(8,128)}) %all-gather.77.cloned.1.call-update) | async-done | bytes 2097168 | tf_op jit(solution)/shard_map/all_gather | solution.py:11
  1200.4 47.8 %all-gather.79.cloned.1.call-done = f32[8,128,512]{2,1,0:T(8,128)} async-done(((f32[1,128,512]{2,1,0:T(8,128)}), f32[8,128,512]{2,1,0:T(8,128)}) %all-gather.79.cloned.1.call-update) | async-done | bytes 2097168 | tf_op jit(solution)/shard_map/all_gather | solution.py:11
  1254.4 11.7 cholesky.358
  1266.2 9.8 custom-call.31
  1278.6 11.9 cholesky.377
  1291.8 9.8 custom-call.32
  1303.2 11.7 cholesky.398
  1315.6 9.8 custom-call.33
  1326.8 11.9 cholesky.415
  1343.2 11.7 while.13
  1354.9 39.3 %custom-call.34 = f32[4,128,128]{1,2,0:T(8,128)S(1)} custom-call(f32[4,128,128]{2,1,0:T(8,128)S(1)} %get-tuple-element.118), custom_call_target="InvertDiagBlocksLowerTriangular" | custom-call | tf_op jit(solution)/shard_map/jit(_solve_triangular)/triangular_solve | solution.py:22
  1405.6 2.8 copy.261
  1421.3 38.2 %all-gather.83.cloned.1.call-done = f32[8,128,512]{2,1,0:T(8,128)} async-done(((f32[1,128,512]{2,1,0:T(8,128)}), f32[8,128,512]{2,1,0:T(8,128)}) %all-gather.83.cloned.1.call-update) | async-done | bytes 2097168 | tf_op jit(solution)/shard_map/all_gather | solution.py:11
  1461.3 48.0 %all-gather.81.cloned.1.call-done = f32[8,128,512]{2,1,0:T(8,128)} async-done(((f32[1,128,512]{2,1,0:T(8,128)}), f32[8,128,512]{2,1,0:T(8,128)}) %all-gather.81.cloned.1.call-update) | async-done | bytes 2097168 | tf_op jit(solution)/shard_map/all_gather | solution.py:11
  1511.1 48.0 %all-gather.85.cloned.1.call-done = f32[8,128,512]{2,1,0:T(8,128)} async-done(((f32[1,128,512]{2,1,0:T(8,128)}), f32[8,128,512]{2,1,0:T(8,128)}) %all-gather.85.cloned.1.call-update) | async-done | bytes 2097168 | tf_op jit(solution)/shard_map/all_gather | solution.py:11
  1560.9 47.8 %all-gather.87.cloned.1.call-done = f32[8,128,512]{2,1,0:T(8,128)} async-done(((f32[1,128,512]{2,1,0:T(8,128)}), f32[8,128,512]{2,1,0:T(8,128)}) %all-gather.87.cloned.1.call-update) | async-done | bytes 2097168 | tf_op jit(solution)/shard_map/all_gather | solution.py:11
  1610.5 48.0 %all-gather.89.cloned.1.call-done = f32[8,128,512]{2,1,0:T(8,128)} async-done(((f32[1,128,512]{2,1,0:T(8,128)}), f32[8,128,512]{2,1,0:T(8,128)}) %all-gather.89.cloned.1.call-update) | async-done | bytes 2097168 | tf_op jit(solution)/shard_map/all_gather | solution.py:11
  1660.3 48.0 %all-gather.91.cloned.1.call-done = f32[8,128,512]{2,1,0:T(8,128)} async-done(((f32[1,128,512]{2,1,0:T(8,128)}), f32[8,128,512]{2,1,0:T(8,128)}) %all-gather.91.cloned.1.call-update) | async-done | bytes 2097168 | tf_op jit(solution)/shard_map/all_gather | solution.py:11
  1710.0 47.8 %all-gather.93.cloned.1.call-done = f32[8,128,512]{2,1,0:T(8,128)} async-done(((f32[1,128,512]{2,1,0:T(8,128)}), f32[8,128,512]{2,1,0:T(8,128)}) %all-gather.93.cloned.1.call-update) | async-done | bytes 2097168 | tf_op jit(solution)/shard_map/all_gather | solution.py:11
  1759.7 48.0 %all-gather.95.cloned.1.call-done = f32[8,128,512]{2,1,0:T(8,128)} async-done(((f32[1,128,512]{2,1,0:T(8,128)}), f32[8,128,512]{2,1,0:T(8,128)}) %all-gather.95.cloned.1.call-update) | async-done | bytes 2097168 | tf_op jit(solution)/shard_map/all_gather | solution.py:11
  1809.5 48.0 %all-gather.97.cloned.1.call-done = f32[8,128,512]{2,1,0:T(8,128)} async-done(((f32[1,128,512]{2,1,0:T(8,128)}), f32[8,128,512]{2,1,0:T(8,128)}) %all-gather.97.cloned.1.call-update) | async-done | bytes 2097168 | tf_op jit(solution)/shard_map/all_gather | solution.py:11
  1857.4 2.5 reduce_sum.358
  1866.4 40.6 %all-gather.99.cloned.1.call-done = f32[8,128,512]{2,1,0:T(8,128)} async-done(((f32[1,128,512]{2,1,0:T(8,128)}), f32[8,128,512]{2,1,0:T(8,128)}) %all-gather.99.cloned.1.call-update) | async-done | bytes 2097168 | tf_op jit(solution)/shard_map/all_gather | solution.py:11
  1909.6 8.3 fusion.4
  1917.9 2.9 fusion.1
  1922.1 3.0 copy.295
  (357 shorter events, 205.2 us)
Async XLA Ops:
  6.5 28.8 %all-gather.101.cloned.1.call-start = ((), (), s32[]{:S(2)}) async-start(), calls=%async_computation.28 | async-start | bytes 1638400 | tf_op jit(solution)/shard_map/all_gather | solution.py:11
  11.5 1.7 copy-start.2
  14.3 40.8 %all-gather.103.cloned.1.call-start = ((), (), s32[]{:S(2)}) async-start(), calls=%async_computation.29 | async-start | bytes 1638400 | tf_op jit(solution)/shard_map/all_gather | solution.py:11
  15.3 59.6 %all-gather.105.cloned.1.call-start = ((), (), s32[]{:S(2)}) async-start(), calls=%async_computation.30 | async-start | bytes 1638400 | tf_op jit(solution)/shard_map/all_gather | solution.py:11
  16.2 78.2 %all-gather.107.cloned.1.call-start = ((), (), s32[]{:S(2)}) async-start(), calls=%async_computation.31 | async-start | bytes 1638400 | tf_op jit(solution)/shard_map/all_gather | solution.py:11
  17.2 129.2 %all-gather.45.cloned.1.call-start = ((), (), s32[]{:S(2)}) async-start(), calls=%async_computation | async-start | bytes 2359296 | tf_op jit(solution)/shard_map/all_gather | solution.py:11
  97.1 98.9 %all-gather.47.cloned.1.call-start = ((), (), s32[]{:S(2)}) async-start(), calls=%async_computation.1 | async-start | bytes 2359296 | tf_op jit(solution)/shard_map/all_gather | solution.py:11
  98.0 147.8 %all-gather.49.cloned.1.call-start = ((), (), s32[]{:S(2)}) async-start(), calls=%async_computation.2 | async-start | bytes 2359296 | tf_op jit(solution)/shard_map/all_gather | solution.py:11
  99.0 196.6 %all-gather.51.cloned.1.call-start = ((), (), s32[]{:S(2)}) async-start(), calls=%async_computation.3 | async-start | bytes 2359296 | tf_op jit(solution)/shard_map/all_gather | solution.py:11
  99.9 407.4 %all-gather.55.cloned.1.call-start = ((), (), s32[]{:S(2)}) async-start(), calls=%async_computation.5 | async-start | bytes 2359296 | tf_op jit(solution)/shard_map/all_gather | solution.py:11
  148.4 149.2 %copy-start.10 = (f32[128,512]{0,1:T(8,128)}, f32[128,512]{0,1:T(8,128)S(1)}, u32[]{:S(2)}) copy-start(f32[128,512]{0,1:T(8,128)S(1)} %copy.184) | copy-start | bytes 786436
  198.0 99.6 %copy-start.11 = (f32[128,512]{0,1:T(8,128)}, f32[128,512]{0,1:T(8,128)S(1)}, u32[]{:S(2)}) copy-start(f32[128,512]{0,1:T(8,128)S(1)} %copy.185) | copy-start | bytes 786436
  247.8 49.8 %copy-start.12 = (f32[128,512]{0,1:T(8,128)}, f32[128,512]{0,1:T(8,128)S(1)}, u32[]{:S(2)}) copy-start(f32[128,512]{0,1:T(8,128)S(1)} %copy.186) | copy-start | bytes 786436
  297.6 0.7 copy-start.13
  300.6 1.0 copy-start.4
  459.5 97.4 %all-gather.53.cloned.1.call-start = ((), (), s32[]{:S(2)}) async-start(), calls=%async_computation.4 | async-start | bytes 2359296 | tf_op jit(solution)/shard_map/all_gather | solution.py:11
  463.0 143.7 %all-gather.57.cloned.1.call-start = ((), (), s32[]{:S(2)}) async-start(), calls=%async_computation.6 | async-start | bytes 2359296 | tf_op jit(solution)/shard_map/all_gather | solution.py:11
  464.9 191.4 %all-gather.59.cloned.1.call-start = ((), (), s32[]{:S(2)}) async-start(), calls=%async_computation.7 | async-start | bytes 2359296 | tf_op jit(solution)/shard_map/all_gather | solution.py:11
  465.8 240.3 %all-gather.61.cloned.1.call-start = ((), (), s32[]{:S(2)}) async-start(), calls=%async_computation.8 | async-start | bytes 2359296 | tf_op jit(solution)/shard_map/all_gather | solution.py:11
  466.7 289.0 %all-gather.63.cloned.1.call-start = ((), (), s32[]{:S(2)}) async-start(), calls=%async_computation.9 | async-start | bytes 2359296 | tf_op jit(solution)/shard_map/all_gather | solution.py:11
  467.7 337.7 %all-gather.65.cloned.1.call-start = ((), (), s32[]{:S(2)}) async-start(), calls=%async_computation.10 | async-start | bytes 2359296 | tf_op jit(solution)/shard_map/all_gather | solution.py:11
  468.6 386.4 %all-gather.67.cloned.1.call-start = ((), (), s32[]{:S(2)}) async-start(), calls=%async_computation.11 | async-start | bytes 2359296 | tf_op jit(solution)/shard_map/all_gather | solution.py:11
  469.5 435.1 %all-gather.69.cloned.1.call-start = ((), (), s32[]{:S(2)}) async-start(), calls=%async_computation.12 | async-start | bytes 2359296 | tf_op jit(solution)/shard_map/all_gather | solution.py:11
  470.4 483.8 %all-gather.71.cloned.1.call-start = ((), (), s32[]{:S(2)}) async-start(), calls=%async_computation.13 | async-start | bytes 2359296 | tf_op jit(solution)/shard_map/all_gather | solution.py:11
  471.5 516.7 %all-gather.109.cloned.1.call-start = ((), (), s32[]{:S(2)}) async-start(), calls=%async_computation.32 | async-start | bytes 1638400 | tf_op jit(solution)/shard_map/all_gather | solution.py:11
  907.1 5.8 copy-start.14
  956.8 8.4 copy-start.3
  968.6 1.7 copy-start
  971.3 36.5 %all-gather.111.cloned.1.call-start = ((), (), s32[]{:S(2)}) async-start(), calls=%async_computation.33 | async-start | bytes 1638400 | tf_op jit(solution)/shard_map/all_gather | solution.py:11
  972.3 55.2 %all-gather.113.cloned.1.call-start = ((), (), s32[]{:S(2)}) async-start(), calls=%async_computation.34 | async-start | bytes 1638400 | tf_op jit(solution)/shard_map/all_gather | solution.py:11
  973.3 74.0 %all-gather.115.cloned.1.call-start = ((), (), s32[]{:S(2)}) async-start(), calls=%async_computation.35 | async-start | bytes 1638400 | tf_op jit(solution)/shard_map/all_gather | solution.py:11
  974.2 125.0 %all-gather.73.cloned.1.call-start = ((), (), s32[]{:S(2)}) async-start(), calls=%async_computation.14 | async-start | bytes 2359296 | tf_op jit(solution)/shard_map/all_gather | solution.py:11
  1050.0 98.9 %all-gather.75.cloned.1.call-start = ((), (), s32[]{:S(2)}) async-start(), calls=%async_computation.15 | async-start | bytes 2359296 | tf_op jit(solution)/shard_map/all_gather | solution.py:11
  1050.9 147.7 %all-gather.77.cloned.1.call-start = ((), (), s32[]{:S(2)}) async-start(), calls=%async_computation.16 | async-start | bytes 2359296 | tf_op jit(solution)/shard_map/all_gather | solution.py:11
  1051.8 196.4 %all-gather.79.cloned.1.call-start = ((), (), s32[]{:S(2)}) async-start(), calls=%async_computation.17 | async-start | bytes 2359296 | tf_op jit(solution)/shard_map/all_gather | solution.py:11
  1052.7 406.7 %all-gather.83.cloned.1.call-start = ((), (), s32[]{:S(2)}) async-start(), calls=%async_computation.19 | async-start | bytes 2359296 | tf_op jit(solution)/shard_map/all_gather | solution.py:11
  1101.0 149.0 %copy-start.6 = (f32[128,512]{1,0:T(8,128)}, f32[128,512]{1,0:T(8,128)S(1)}, u32[]{:S(2)}) copy-start(f32[128,512]{1,0:T(8,128)S(1)} %reduce_sum.346) | copy-start | bytes 786436
  1150.7 99.4 %copy-start.7 = (f32[128,512]{1,0:T(8,128)}, f32[128,512]{1,0:T(8,128)S(1)}, u32[]{:S(2)}) copy-start(f32[128,512]{1,0:T(8,128)S(1)} %reduce_sum.347) | copy-start | bytes 786436
  1200.4 49.7 %copy-start.8 = (f32[128,512]{1,0:T(8,128)}, f32[128,512]{1,0:T(8,128)S(1)}, u32[]{:S(2)}) copy-start(f32[128,512]{1,0:T(8,128)S(1)} %reduce_sum.348) | copy-start | bytes 786436
  1250.1 0.7 copy-start.9
  1253.4 1.0 copy-start.5
  1411.7 97.5 %all-gather.81.cloned.1.call-start = ((), (), s32[]{:S(2)}) async-start(), calls=%async_computation.18 | async-start | bytes 2359296 | tf_op jit(solution)/shard_map/all_gather | solution.py:11
  1412.7 146.4 %all-gather.85.cloned.1.call-start = ((), (), s32[]{:S(2)}) async-start(), calls=%async_computation.20 | async-start | bytes 2359296 | tf_op jit(solution)/shard_map/all_gather | solution.py:11
  1414.5 194.1 %all-gather.87.cloned.1.call-start = ((), (), s32[]{:S(2)}) async-start(), calls=%async_computation.21 | async-start | bytes 2359296 | tf_op jit(solution)/shard_map/all_gather | solution.py:11
  1415.5 243.0 %all-gather.89.cloned.1.call-start = ((), (), s32[]{:S(2)}) async-start(), calls=%async_computation.22 | async-start | bytes 2359296 | tf_op jit(solution)/shard_map/all_gather | solution.py:11
  1416.4 291.8 %all-gather.91.cloned.1.call-start = ((), (), s32[]{:S(2)}) async-start(), calls=%async_computation.23 | async-start | bytes 2359296 | tf_op jit(solution)/shard_map/all_gather | solution.py:11
  1417.3 340.5 %all-gather.93.cloned.1.call-start = ((), (), s32[]{:S(2)}) async-start(), calls=%async_computation.24 | async-start | bytes 2359296 | tf_op jit(solution)/shard_map/all_gather | solution.py:11
  1418.2 389.4 %all-gather.95.cloned.1.call-start = ((), (), s32[]{:S(2)}) async-start(), calls=%async_computation.25 | async-start | bytes 2359296 | tf_op jit(solution)/shard_map/all_gather | solution.py:11
  1419.2 438.2 %all-gather.97.cloned.1.call-start = ((), (), s32[]{:S(2)}) async-start(), calls=%async_computation.26 | async-start | bytes 2359296 | tf_op jit(solution)/shard_map/all_gather | solution.py:11
  1420.1 487.0 %all-gather.99.cloned.1.call-start = ((), (), s32[]{:S(2)}) async-start(), calls=%async_computation.27 | async-start | bytes 2359296 | tf_op jit(solution)/shard_map/all_gather | solution.py:11
  1859.9 5.8 copy-start.15
  1909.6 8.3 copy-start.1
Sparse Core Ops, SparseCore 0:
  14.4 20.8 all-gather.100
  36.9 18.1 all-gather.102
  56.6 18.1 all-gather.104
  76.3 18.1 all-gather.106
  97.2 49.1 all-gather.44
  148.4 47.6 all-gather.46
  198.2 47.6 all-gather.48
  247.9 47.6 all-gather.50
  459.6 47.6 all-gather.54
  509.2 47.6 all-gather.52
  559.0 47.6 all-gather.56
  608.7 47.6 all-gather.58
  658.4 47.6 all-gather.60
  708.1 47.6 all-gather.62
  757.7 47.6 all-gather.64
  807.3 47.6 all-gather.66
  856.9 47.6 all-gather.68
  906.6 47.6 all-gather.70
  971.5 16.6 all-gather.108
  989.6 18.1 all-gather.110
  1009.4 18.1 all-gather.112
  1029.1 18.1 all-gather.114
  1050.1 49.0 all-gather.72
  1101.2 47.6 all-gather.74
  1151.0 47.6 all-gather.76
  1200.6 47.6 all-gather.78
  1411.8 47.5 all-gather.82
  1461.6 47.6 all-gather.80
  1511.4 47.6 all-gather.84
  1561.0 47.6 all-gather.86
  1610.8 47.6 all-gather.88
  1660.6 47.6 all-gather.90
  1710.2 47.6 all-gather.92
  1760.0 47.6 all-gather.94
  1809.8 47.6 all-gather.96
  1859.4 47.6 all-gather.98
